TPU v7x, 32 devices: a whole 2x2x4 slice. The times are simulated.
32 devices in a mesh: cluster: 8 (over z, y), sub: 4 (over x, core).
Axes of the slice: x: 2, y: 2, z: 4, core: 2. Of those that a mesh axis runs over, the one named last changes fastest.
Arguments:
- right_side: float32 [4, 8, 16, 384], P('sub', 'cluster'), may hold values from -12 to 12
- schur: float32 [4, 8, 768, 768], P('sub', 'cluster'), as said below
- rigid_modes: float32 [4, 8, 6, 768], P('sub', 'cluster'), may hold values from -0.21875 to 0.21875
- mode_count: int32 [4, 8], P('sub', 'cluster'), may hold values from 3 to 6
- face_order: int32 [4, 8, 384], P('sub', 'cluster'), may hold values from 0 to 383, each once within a row
- dual_scale: float32 [4, 8, 384], P('sub', 'cluster'), may hold values from 0.5 to 2
- rigid_loads: float32 [4, 8, 6, 16], P('sub', 'cluster'), may hold values from -6 to 6
- coarse_inverse: float32 [192, 192], P(('cluster', 'sub')), as said below
Outputs:
- multipliers: float32 [4, 8, 16, 384], P('sub', 'cluster')
- residual: float32 [4, 8, 16, 384], P('sub', 'cluster')
Inputs may be any that keep to these rules, and one draw needn't show every extreme that they name: rigid-body modes m with m >= mode_count are unused. `face_order`: each subdomain's entries form a permutation of the face unknowns; those of the first subdomain of a chain are unused. `schur`: each subdomain's matrix is symmetric. `coarse_inverse`: symmetric.
All inputs are finite; a program needn't handle non-finite values.
Results may differ from a plain program's by a relative error of at most 0.0003.
Values sent between devices are 32-bit elements; how exact they have to be, the bound alone decides.
No kernel may reach another device: no remote copies, remote signals or barrier semaphores. Data moves between devices by JAX's collectives and lax.ppermute only.
A program may use at most 64 MiB of HBM per device.

v0:
```python
import jax
import jax.numpy as jnp
from jax import lax
from jax.sharding import PartitionSpec as P

ITERS = 2
highest = lax.Precision.HIGHEST


def from_behind(block, axis, distance):
    devices = range(lax.axis_size(axis))
    route = [(i - distance, i) for i in devices if i - distance in devices]
    return lax.ppermute(block, axis, route)


def permute_faces(field, index):

    def single_face(values, order):
        return jnp.take(values, order, axis=1)

    return jax.vmap(jax.vmap(single_face))(field, index)


def lift_faces(dual_field, face_order):
    incoming = from_behind(dual_field, "cluster", 1)
    earlier = jnp.concatenate([incoming, dual_field[:, :-1]], axis=1)
    left_face = -permute_faces(earlier, face_order)
    return jnp.concatenate([left_face, dual_field], axis=3)


def push_faces(values, inverse):
    half_size = values.shape[3] // 2
    left_face = values[..., :half_size]
    right_face = values[..., half_size:]
    returned = -permute_faces(left_face, inverse)
    outgoing = from_behind(returned, "cluster", -1)
    following = jnp.concatenate([returned[:, 1:], outgoing], axis=1)
    return right_face + following


def apply_dual(dual_field, schur, face_order, inverse):
    lifted = lift_faces(dual_field, face_order)
    dual_image = jnp.einsum("sjci,sjik->sjck", lifted, schur, precision=highest)
    return push_faces(dual_image, inverse)


def basis_transpose(dual_field, basis, face_order):
    return jnp.einsum(
        "sjmi,sjci->sjmc", basis, lift_faces(dual_field, face_order), precision=highest
    )


def basis_expand(coefficients, basis, inverse):
    return push_faces(
        jnp.einsum("sjmi,sjmc->sjci", basis, coefficients, precision=highest), inverse
    )


def coarse_plain(coefficients, coarse_rows):
    flattened = coefficients.reshape(-1, coefficients.shape[3])
    solved = lax.psum_scatter(
        jnp.dot(coarse_rows.T, flattened, precision=highest),
        ("cluster", "sub"),
        scatter_dimension=0,
        tiled=True,
    )
    return solved.reshape(coefficients.shape)


def project(dual_field, basis, face_order, inverse, coarse_rows):
    coefficients = basis_transpose(dual_field, basis, face_order)
    return dual_field - basis_expand(coarse_plain(coefficients, coarse_rows), basis, inverse)


def gram_product(first_field, second_field):
    return jnp.einsum("sjcm,sjdm->cd", first_field, second_field, precision=highest)


def solve_small(matrix, right_hand):
    factor = jnp.linalg.cholesky(matrix)
    halfway = lax.linalg.triangular_solve(factor, right_hand, left_side=True, lower=True)
    return lax.linalg.triangular_solve(
        factor, halfway, left_side=True, lower=True, transpose_a=True
    )


def step_quantities(dual_image, direction, residual, basis, face_order, inverse, coarse_rows):
    curvature_part = gram_product(direction, dual_image)
    descent_part = gram_product(direction, residual)
    coefficients = basis_transpose(dual_image, basis, face_order)
    curvature, descent = lax.psum((curvature_part, descent_part), ("cluster", "sub"))
    solved = coarse_plain(coefficients, coarse_rows)
    projected_image = dual_image - basis_expand(solved, basis, inverse)
    return (curvature, descent, projected_image)


def shards(
    right_side, schur, rigid_modes, mode_count, face_order, dual_scale, rigid_loads, coarse_inverse
):
    inverse = jnp.argsort(face_order, axis=-1)
    active = (jnp.arange(rigid_modes.shape[2])[None, None, :] < mode_count[:, :, None]).astype(
        jnp.float32
    )
    basis = rigid_modes * active[..., None]
    masked_loads = rigid_loads * active[..., None]
    scaling = dual_scale[:, :, None, :]
    multipliers = basis_expand(coarse_plain(masked_loads, coarse_inverse), basis, inverse)
    residual = project(
        right_side - apply_dual(multipliers, schur, face_order, inverse),
        basis,
        face_order,
        inverse,
        coarse_inverse,
    )
    search = project(scaling * residual, basis, face_order, inverse, coarse_inverse)
    direction = search
    for iteration in range(ITERS):
        dual_image = apply_dual(direction, schur, face_order, inverse)
        curvature, descent, projected_image = step_quantities(
            dual_image, direction, residual, basis, face_order, inverse, coarse_inverse
        )
        step_size = solve_small(curvature, descent)
        multipliers = multipliers + jnp.einsum(
            "sjcm,cd->sjdm", direction, step_size, precision=highest
        )
        residual = residual - jnp.einsum(
            "sjcm,cd->sjdm", projected_image, step_size, precision=highest
        )
        if iteration + 1 < ITERS:
            search = project(scaling * residual, basis, face_order, inverse, coarse_inverse)
            update = lax.psum(gram_product(dual_image, search), ("cluster", "sub"))
            correction = -solve_small(curvature, update)
            direction = search + jnp.einsum(
                "sjcm,cd->sjdm", direction, correction, precision=highest
            )
    return (multipliers, residual)


def solution(mesh):
    in_specs = (
        P("sub", "cluster", None, None),
        P("sub", "cluster", None, None),
        P("sub", "cluster", None, None),
        P("sub", "cluster"),
        P("sub", "cluster", None),
        P("sub", "cluster", None),
        P("sub", "cluster", None, None),
        P(("cluster", "sub"), None),
    )
    out_specs = (P("sub", "cluster", None, None), P("sub", "cluster", None, None))
    return jax.shard_map(shards, mesh=mesh, in_specs=in_specs, out_specs=out_specs, check_vma=False)
```

profile of v0, /device:TPU:6, one launch (start us, length us, event | category | flops | bytes accessed | tf_op | source)
XLA Modules:
  0.0 495.1 jit_solution(11295149442735976061)
XLA Ops:
  9.6 40.4 %all-reduce = f32[192,16]{0,1:T(8,128)S(1)} all-reduce(f32[192,16]{0,1:T(8,128)S(1)} %convolution_bitcast_fusion.16), channel_id=2, replica_groups=mesh['cluster'=8,'sub'=4] {'cluster','sub'}, use_global_device_ids=true, to_apply=%region_0.0.clone | all-reduce | flops 3072 | bytes 24576
  69.1 3.8 gather_fusion.1
  74.5 3.8 gather_fusion.2
  80.4 4.7 collective-permute-done.2
  90.9 3.8 gather_fusion.3
  95.3 41.6 %all-reduce.1 = f32[192,16]{0,1:T(8,128)S(1)} all-reduce(f32[192,16]{0,1:T(8,128)S(1)} %convolution_bitcast_fusion.15), channel_id=3, replica_groups=mesh['cluster'=8,'sub'=4] {'cluster','sub'}, use_global_device_ids=true, to_apply=%region_2.4.clone | all-reduce | flops 3072 | bytes 24576
  137.2 3.8 gather_fusion.4
  143.7 4.1 collective-permute-done.4
  153.7 3.8 gather_fusion.5
  158.0 39.5 %all-reduce.2 = f32[192,16]{0,1:T(8,128)S(1)} all-reduce(f32[192,16]{0,1:T(8,128)S(1)} %convolution_bitcast_fusion.14), channel_id=4, replica_groups=mesh['cluster'=8,'sub'=4] {'cluster','sub'}, use_global_device_ids=true, to_apply=%region_3.5.clone | all-reduce | flops 3072 | bytes 24576
  197.9 3.8 gather_fusion.6
  214.4 3.8 gather_fusion.7
  219.7 3.8 gather_fusion.8
  225.7 4.6 collective-permute-done.8
  236.2 3.8 gather_fusion.9
  240.5 40.7 %all-reduce.7 = (f32[16,16]{1,0:T(8,128)S(1)}, f32[16,16]{0,1:T(8,128)S(1)}, f32[192,16]{0,1:T(8,128)S(1)}) all-reduce(f32[16,16]{1,0:T(8,128)S(1)} %fusion.99, f32[16,16]{0,1:T(8,128)S(1)} %fusion.102, f32[192,16]{0,1:T(8,128)S(1)} %convolution_bitcast_fusion.13), channel_id=1, replica_groups=mesh['cluster'=8,'sub'=4] {'cluster','sub'}, use_global_device_ids=true, to_apply=%region_7.10 | all-reduce | flops 3584 | bytes 28672 | tf_op jit(solution)/shard_map/psum | solution.py:91
  285.8 3.8 gather_fusion.10
  302.4 3.8 gather_fusion.11
  306.8 39.6 %all-reduce.4 = f32[192,16]{0,1:T(8,128)S(1)} all-reduce(f32[192,16]{0,1:T(8,128)S(1)} %convolution_bitcast_fusion.12), channel_id=6, replica_groups=mesh['cluster'=8,'sub'=4] {'cluster','sub'}, use_global_device_ids=true, to_apply=%region_9.0.clone | all-reduce | flops 3072 | bytes 24576
  346.8 3.8 gather_fusion.12
  357.5 40.5 %psum.37 = f32[16,16]{1,0:T(8,128)S(1)} all-reduce(f32[16,16]{1,0:T(8,128)S(1)} %fusion.97), channel_id=1, replica_groups=mesh['cluster'=8,'sub'=4] {'cluster','sub'}, use_global_device_ids=true, to_apply=%region_10.0 | all-reduce | flops 256 | bytes 2048 | tf_op jit(solution)/shard_map/psum | solution.py:131
  415.8 4.5 collective-permute-done.14
  426.2 3.8 gather_fusion.15
  430.6 40.7 %all-reduce.6 = (f32[16,16]{1,0:T(8,128)S(1)}, f32[16,16]{0,1:T(8,128)S(1)}, f32[192,16]{0,1:T(8,128)S(1)}) all-reduce(f32[16,16]{1,0:T(8,128)S(1)} %fusion.90, f32[16,16]{0,1:T(8,128)S(1)} %fusion.92, f32[192,16]{0,1:T(8,128)S(1)} %convolution_bitcast_fusion.11), channel_id=1, replica_groups=mesh['cluster'=8,'sub'=4] {'cluster','sub'}, use_global_device_ids=true, to_apply=%region_12.0 | all-reduce | flops 3584 | bytes 28672 | tf_op jit(solution)/shard_map/psum | solution.py:91
  (172 shorter events, 128.1 us)
Async XLA Ops:
  7.2 65.9 %copy-start = (f32[1,1,768,768]{3,2,1,0:T(8,128)S(1)}, f32[1,1,768,768]{3,2,1,0:T(8,128)}, u32[]{:S(2)}) copy-start(f32[1,1,768,768]{3,2,1,0:T(8,128)} %param.16) | copy-start | bytes 7077892
  7.2 44.1 %sort.19.cloned.1.call-start = ((), (), s32[]{:S(2)}) async-start(), calls=%async_computation | async-start | bytes 9248 | tf_op jit(solution)/shard_map/jit(argsort)/sort | solution.py:100
  56.5 28.5 %copy-start.2 = (f32[1,1,16,384]{3,2,1,0:T(8,128)S(1)}, f32[1,1,16,384]{3,2,1,0:T(8,128)}, u32[]{:S(2)}) copy-start(f32[1,1,16,384]{3,2,1,0:T(8,128)} %param.15) | copy-start | bytes 73732
  56.6 6.6 %collective-permute-start = (f32[1,1,16,384]{3,2,1,0:T(8,128)S(1)}, f32[1,1,16,384]{3,2,1,0:T(8,128)S(1)}, u32[]{:S(2)}, u32[]{:S(2)}) collective-permute-start(f32[1,1,16,384]{3,2,1,0:T(8,128)S(1)} %fusion.89), channel_id=1, source_target_pairs={{4,0},{8,4},{12,8},{16,12},{20,16},{24,20},{28,24},{5,1},{9,5},{13... | collective-permute-start | bytes 73736 | tf_op jit(solution)/shard_map/ppermute | solution.py:13
  63.3 5.7 %collective-permute-start.1 = (f32[1,1,16,384]{3,2,1,0:T(8,128)S(1)}, f32[1,1,16,384]{3,2,1,0:T(8,128)S(1)}, u32[]{:S(2)}, u32[]{:S(2)}) collective-permute-start(f32[1,1,16,384]{3,2,1,0:T(8,128)S(1)} %slice_add_fusion.8), channel_id=1, source_target_pairs={{0,4},{4,8},{8,12},{12,16},{16,20},{20,24},{24,28},{1,5},{5,9},{9,... | collective-permute-start | bytes 73736 | tf_op jit(solution)/shard_map/ppermute | solution.py:13
  73.0 22.1 %copy-start.1 = (f32[6,192]{1,0:T(8,128)S(1)}, f32[6,192]{1,0:T(8,128)}, u32[]{:S(2)}) copy-start(f32[6,192]{1,0:T(8,128)} %param.22) | copy-start | bytes 13828
  73.1 70.6 %copy-start.3 = (f32[1,1,384]{2,1,0:T(1,128)S(1)}, f32[1,1,384]{2,1,0:T(1,128)}, u32[]{:S(2)}) copy-start(f32[1,1,384]{2,1,0:T(1,128)} %param.20) | copy-start | bytes 4612
  78.4 6.6 %collective-permute-start.2 = (f32[1,1,16,384]{3,2,1,0:T(8,128)S(1)}, f32[1,1,16,384]{3,2,1,0:T(8,128)S(1)}, u32[]{:S(2)}, u32[]{:S(2)}) collective-permute-start(f32[1,1,16,384]{3,2,1,0:T(8,128)S(1)} %fusion.87), channel_id=1, source_target_pairs={{4,0},{8,4},{12,8},{16,12},{20,16},{24,20},{28,24},{5,1},{9,5},{13... | collective-permute-start | bytes 73736 | tf_op jit(solution)/shard_map/ppermute | solution.py:13
  85.1 5.7 %collective-permute-start.3 = (f32[1,1,16,384]{3,2,1,0:T(8,128)S(1)}, f32[1,1,16,384]{3,2,1,0:T(8,128)S(1)}, u32[]{:S(2)}, u32[]{:S(2)}) collective-permute-start(f32[1,1,16,384]{3,2,1,0:T(8,128)S(1)} %fusion.50), channel_id=1, source_target_pairs={{0,4},{4,8},{8,12},{12,16},{16,20},{20,24},{24,28},{1,5},{5,9},{9,... | collective-permute-start | bytes 73736 | tf_op jit(solution)/shard_map/ppermute | solution.py:13
  141.2 6.6 %collective-permute-start.4 = (f32[1,1,16,384]{3,2,1,0:T(8,128)S(1)}, f32[1,1,16,384]{3,2,1,0:T(8,128)S(1)}, u32[]{:S(2)}, u32[]{:S(2)}) collective-permute-start(f32[1,1,16,384]{3,2,1,0:T(8,128)S(1)} %fusion.85), channel_id=1, source_target_pairs={{4,0},{8,4},{12,8},{16,12},{20,16},{24,20},{28,24},{5,1},{9,5},{13... | collective-permute-start | bytes 73736 | tf_op jit(solution)/shard_map/ppermute | solution.py:13
  147.8 5.7 %collective-permute-start.5 = (f32[1,1,16,384]{3,2,1,0:T(8,128)S(1)}, f32[1,1,16,384]{3,2,1,0:T(8,128)S(1)}, u32[]{:S(2)}, u32[]{:S(2)}) collective-permute-start(f32[1,1,16,384]{3,2,1,0:T(8,128)S(1)} %get-tuple-element.14), channel_id=1, source_target_pairs={{0,4},{4,8},{8,12},{12,16},{16,20},{20,24},{24,28},{1,5},{5,9},{9,... | collective-permute-start | bytes 73736 | tf_op jit(solution)/shard_map/ppermute | solution.py:13
  201.9 6.6 %collective-permute-start.6 = (f32[1,1,16,384]{3,2,1,0:T(8,128)S(1)}, f32[1,1,16,384]{3,2,1,0:T(8,128)S(1)}, u32[]{:S(2)}, u32[]{:S(2)}) collective-permute-start(f32[1,1,16,384]{3,2,1,0:T(8,128)S(1)} %fusion.83), channel_id=1, source_target_pairs={{4,0},{8,4},{12,8},{16,12},{20,16},{24,20},{28,24},{5,1},{9,5},{13... | collective-permute-start | bytes 73736 | tf_op jit(solution)/shard_map/ppermute | solution.py:13
  208.5 5.7 %collective-permute-start.7 = (f32[1,1,16,384]{3,2,1,0:T(8,128)S(1)}, f32[1,1,16,384]{3,2,1,0:T(8,128)S(1)}, u32[]{:S(2)}, u32[]{:S(2)}) collective-permute-start(f32[1,1,16,384]{3,2,1,0:T(8,128)S(1)} %fusion.48), channel_id=1, source_target_pairs={{0,4},{4,8},{8,12},{12,16},{16,20},{20,24},{24,28},{1,5},{5,9},{9,... | collective-permute-start | bytes 73736 | tf_op jit(solution)/shard_map/ppermute | solution.py:13
  223.6 6.7 %collective-permute-start.8 = (f32[1,1,16,384]{3,2,1,0:T(8,128)S(1)}, f32[1,1,16,384]{3,2,1,0:T(8,128)S(1)}, u32[]{:S(2)}, u32[]{:S(2)}) collective-permute-start(f32[1,1,16,384]{3,2,1,0:T(8,128)S(1)} %fusion.81), channel_id=1, source_target_pairs={{4,0},{8,4},{12,8},{16,12},{20,16},{24,20},{28,24},{5,1},{9,5},{13... | collective-permute-start | bytes 73736 | tf_op jit(solution)/shard_map/ppermute | solution.py:13
  230.4 5.7 %collective-permute-start.9 = (f32[1,1,16,384]{3,2,1,0:T(8,128)S(1)}, f32[1,1,16,384]{3,2,1,0:T(8,128)S(1)}, u32[]{:S(2)}, u32[]{:S(2)}) collective-permute-start(f32[1,1,16,384]{3,2,1,0:T(8,128)S(1)} %slice_add_fusion.4), channel_id=1, source_target_pairs={{0,4},{4,8},{8,12},{12,16},{16,20},{20,24},{24,28},{1,5},{5,9},{9,... | collective-permute-start | bytes 73736 | tf_op jit(solution)/shard_map/ppermute | solution.py:13
  289.7 6.6 %collective-permute-start.10 = (f32[1,1,16,384]{3,2,1,0:T(8,128)S(1)}, f32[1,1,16,384]{3,2,1,0:T(8,128)S(1)}, u32[]{:S(2)}, u32[]{:S(2)}) collective-permute-start(f32[1,1,16,384]{3,2,1,0:T(8,128)S(1)} %fusion.79), channel_id=1, source_target_pairs={{4,0},{8,4},{12,8},{16,12},{20,16},{24,20},{28,24},{5,1},{9,5},{13... | collective-permute-start | bytes 73736 | tf_op jit(solution)/shard_map/ppermute | solution.py:13
  296.6 5.7 %collective-permute-start.11 = (f32[1,1,16,384]{3,2,1,0:T(8,128)S(1)}, f32[1,1,16,384]{3,2,1,0:T(8,128)S(1)}, u32[]{:S(2)}, u32[]{:S(2)}) collective-permute-start(f32[1,1,16,384]{3,2,1,0:T(8,128)S(1)} %get-tuple-element.18), channel_id=1, source_target_pairs={{0,4},{4,8},{8,12},{12,16},{16,20},{20,24},{24,28},{1,5},{5,9},{9,... | collective-permute-start | bytes 73736 | tf_op jit(solution)/shard_map/ppermute | solution.py:13
  350.7 6.6 %collective-permute-start.12 = (f32[1,1,16,384]{3,2,1,0:T(8,128)S(1)}, f32[1,1,16,384]{3,2,1,0:T(8,128)S(1)}, u32[]{:S(2)}, u32[]{:S(2)}) collective-permute-start(f32[1,1,16,384]{3,2,1,0:T(8,128)S(1)} %fusion.77), channel_id=1, source_target_pairs={{4,0},{8,4},{12,8},{16,12},{20,16},{24,20},{28,24},{5,1},{9,5},{13... | collective-permute-start | bytes 73736 | tf_op jit(solution)/shard_map/ppermute | solution.py:13
  398.6 5.7 %collective-permute-start.13 = (f32[1,1,16,384]{3,2,1,0:T(8,128)S(1)}, f32[1,1,16,384]{3,2,1,0:T(8,128)S(1)}, u32[]{:S(2)}, u32[]{:S(2)}) collective-permute-start(f32[1,1,16,384]{3,2,1,0:T(8,128)S(1)} %fusion.18), channel_id=1, source_target_pairs={{0,4},{4,8},{8,12},{12,16},{16,20},{20,24},{24,28},{1,5},{5,9},{9,... | collective-permute-start | bytes 73736 | tf_op jit(solution)/shard_map/ppermute | solution.py:13
  413.7 6.6 %collective-permute-start.14 = (f32[1,1,16,384]{3,2,1,0:T(8,128)S(1)}, f32[1,1,16,384]{3,2,1,0:T(8,128)S(1)}, u32[]{:S(2)}, u32[]{:S(2)}) collective-permute-start(f32[1,1,16,384]{3,2,1,0:T(8,128)S(1)} %fusion.75), channel_id=1, source_target_pairs={{4,0},{8,4},{12,8},{16,12},{20,16},{24,20},{28,24},{5,1},{9,5},{13... | collective-permute-start | bytes 73736 | tf_op jit(solution)/shard_map/ppermute | solution.py:13
  420.4 5.7 %collective-permute-start.15 = (f32[1,1,16,384]{3,2,1,0:T(8,128)S(1)}, f32[1,1,16,384]{3,2,1,0:T(8,128)S(1)}, u32[]{:S(2)}, u32[]{:S(2)}) collective-permute-start(f32[1,1,16,384]{3,2,1,0:T(8,128)S(1)} %slice_add_fusion.1), channel_id=1, source_target_pairs={{0,4},{4,8},{8,12},{12,16},{16,20},{20,24},{24,28},{1,5},{5,9},{9,... | collective-permute-start | bytes 73736 | tf_op jit(solution)/shard_map/ppermute | solution.py:13
  480.3 6.6 %collective-permute-start.16 = (f32[1,1,16,384]{3,2,1,0:T(8,128)S(1)}, f32[1,1,16,384]{3,2,1,0:T(8,128)S(1)}, u32[]{:S(2)}, u32[]{:S(2)}) collective-permute-start(f32[1,1,16,384]{3,2,1,0:T(8,128)S(1)} %fusion.73), channel_id=1, source_target_pairs={{4,0},{8,4},{12,8},{16,12},{20,16},{24,20},{28,24},{5,1},{9,5},{13... | collective-permute-start | bytes 73736 | tf_op jit(solution)/shard_map/ppermute | solution.py:13
Sparse Core Ops, SparseCore 0:
  10.9 2.7 sort.21.cloned.1.call-done
  (1 shorter events, 0.0 us)
where the time goes:
time: 504 us; the launch traced here: 495 us
  blocking collectives  283 us (56%)
  local copies, waits for them, and re-layouts  69.8 us (14%)
  waiting for transfers between devices  57.6 us (11%)
  starting transfers between devices  45.2 us (9%)
  between operations  15.9 us (3%)
  matrix products  12.3 us (2%)
  other arithmetic  11.2 us (2%)
    unnamed x4, blocking collectives  161 us
    psum x2, blocking collectives, step_quantities(): lax.psum((curvature_part, descent_part), ('cluster', 'sub'))  81.4 us
    gather x34, local copies, waits for them, and re-layouts, single_face(): return jnp.take(values, order, axis=1)  66.8 us
    ppermute x17, waiting for transfers between devices, from_behind(): return lax.ppermute(block, axis, route)  57.6 us
    ppermute x17, starting transfers between devices, from_behind(): return lax.ppermute(block, axis, route)  45.2 us
    psum x1, blocking collectives, shards(): update = lax.psum(gram_product(dual_image, search), ('cluster', 'sub'))  40.5 us
  transfers between devices with their start and end apart: 17, of which 17 were waited for; matrix products, arithmetic and copies ran while one was open for 1% of the time, Pallas kernels for 0%

commit v1 on v0

--- a/solution.py
+++ b/solution.py
@@ -88,7 +88,7 @@
     curvature_part = gram_product(direction, dual_image)
     descent_part = gram_product(direction, residual)
     coefficients = basis_transpose(dual_image, basis, face_order)
-    curvature, descent = lax.psum((curvature_part, descent_part), ("cluster", "sub"))
+    curvature, descent = lax.psum(lax.psum((curvature_part, descent_part), "sub"), "cluster")
     solved = coarse_plain(coefficients, coarse_rows)
     projected_image = dual_image - basis_expand(solved, basis, inverse)
     return (curvature, descent, projected_image)

time: 504 us -> 585 us (1.16)
  blocking collectives: 283 us -> 367 us
  waiting for transfers between devices: 57.6 us -> 50.1 us
    unnamed x4 -> x6, blocking collectives: 161 us -> 245 us
    ppermute x17, waiting for transfers between devices: 57.6 us -> 50.1 us  [from_behind(): return lax.ppermute(block, axis, route)]
    psum x2 -> x4, blocking collectives: 81.4 us -> 82.2 us  [the longest x2 61.9 us: step_quantities(): lax.psum(lax.psum((curvature_part, descent_part), 'sub'), 'cluster')]
  transfers between devices with their start and end apart: 17 -> 17, of which waited for: 17 -> 15; matrix products, arithmetic and copies ran while one was open for 1% -> 2% of each run, Pallas kernels for 0% -> 0%
where the time goes in v1:
time: 585 us; the launch traced here: 575 us
  blocking collectives  367 us (63%)
  local copies, waits for them, and re-layouts  69.8 us (12%)
  waiting for transfers between devices  50.1 us (9%)
  starting transfers between devices  48.5 us (8%)
  between operations  15.9 us (3%)
  matrix products  12.3 us (2%)
  other arithmetic  11.2 us (2%)
    unnamed x6, blocking collectives  245 us
    gather x34, local copies, waits for them, and re-layouts, single_face(): return jnp.take(values, order, axis=1)  66.8 us
    psum x2, blocking collectives, step_quantities(): lax.psum(lax.psum((curvature_part, descent_part), 'sub'), 'cluster')  61.9 us
    ppermute x17, waiting for transfers between devices, from_behind(): return lax.ppermute(block, axis, route)  50.1 us
    ppermute x17, starting transfers between devices, from_behind(): return lax.ppermute(block, axis, route)  48.5 us
    psum x1, blocking collectives, shards(): update = lax.psum(gram_product(dual_image, search), ('cluster', 'sub'))  39.7 us
    psum x2, blocking collectives, step_quantities(): lax.psum((curvature_part, descent_part), 'sub')  20.3 us
  transfers between devices with their start and end apart: 17, of which 15 were waited for; matrix products, arithmetic and copies ran while one was open for 2% of the time, Pallas kernels for 0%

profile of v1, /device:TPU:6, one launch (start us, length us, event | category | flops | bytes accessed | tf_op | source)
XLA Modules:
  0.0 574.9 jit_solution(12891280061495667047)
XLA Ops:
  9.6 40.4 %all-reduce = f32[192,16]{0,1:T(8,128)S(1)} all-reduce(f32[192,16]{0,1:T(8,128)S(1)} %convolution_bitcast_fusion.16), channel_id=2, replica_groups=mesh['cluster'=8,'sub'=4] {'cluster','sub'}, use_global_device_ids=true, to_apply=%region_0.0.clone | all-reduce | flops 3072 | bytes 24576
  74.5 3.8 gather_fusion.2
  80.4 4.7 collective-permute-done.2
  90.9 3.8 gather_fusion.3
  95.3 41.6 %all-reduce.1 = f32[192,16]{0,1:T(8,128)S(1)} all-reduce(f32[192,16]{0,1:T(8,128)S(1)} %convolution_bitcast_fusion.15), channel_id=3, replica_groups=mesh['cluster'=8,'sub'=4] {'cluster','sub'}, use_global_device_ids=true, to_apply=%region_2.4.clone | all-reduce | flops 3072 | bytes 24576
  137.2 3.8 gather_fusion.4
  143.7 4.1 collective-permute-done.4
  153.7 3.8 gather_fusion.5
  158.0 39.5 %all-reduce.2 = f32[192,16]{0,1:T(8,128)S(1)} all-reduce(f32[192,16]{0,1:T(8,128)S(1)} %convolution_bitcast_fusion.14), channel_id=4, replica_groups=mesh['cluster'=8,'sub'=4] {'cluster','sub'}, use_global_device_ids=true, to_apply=%region_3.5.clone | all-reduce | flops 3072 | bytes 24576
  197.9 3.8 gather_fusion.6
  225.7 4.6 collective-permute-done.8
  233.4 10.1 %all-reduce.9 = (f32[16,16]{1,0:T(8,128)S(1)}, f32[16,16]{0,1:T(8,128)S(1)}) all-reduce(f32[16,16]{1,0:T(8,128)S(1)} %fusion.99, f32[16,16]{0,1:T(8,128)S(1)} %fusion.102), channel_id=1, replica_groups=mesh['cluster'=8,'sub'=4] {'sub'}, use_global_device_ids=true, to_apply=%region_8.11 | all-reduce | flops 512 | bytes 4096 | tf_op jit(solution)/shard_map/psum | solution.py:91
  243.6 31.1 %all-reduce.7 = (f32[16,16]{1,0:T(8,128)S(1)}, f32[16,16]{0,1:T(8,128)S(1)}) all-reduce(f32[16,16]{1,0:T(8,128)S(1)} %get-tuple-element.14, f32[16,16]{0,1:T(8,128)S(1)} %get-tuple-element.15), channel_id=1, replica_groups=mesh['cluster'=8,'sub'=4] {'cluster'}, use_global_device_ids=true, to_apply=%region_9.12 | all-reduce | flops 512 | bytes 4096 | tf_op jit(solution)/shard_map/psum | solution.py:91
  279.1 3.8 gather_fusion.9
  283.5 40.9 %all-reduce.3 = f32[192,16]{0,1:T(8,128)S(1)} all-reduce(f32[192,16]{0,1:T(8,128)S(1)} %convolution_bitcast_fusion.13), channel_id=5, replica_groups=mesh['cluster'=8,'sub'=4] {'cluster','sub'}, use_global_device_ids=true, to_apply=%region_10.0.clone | all-reduce | flops 3072 | bytes 24576
  324.8 3.8 gather_fusion.10
  331.1 4.3 collective-permute-done.10
  345.8 41.1 %all-reduce.4 = f32[192,16]{0,1:T(8,128)S(1)} all-reduce(f32[192,16]{0,1:T(8,128)S(1)} %convolution_bitcast_fusion.12), channel_id=6, replica_groups=mesh['cluster'=8,'sub'=4] {'cluster','sub'}, use_global_device_ids=true, to_apply=%region_11.0.clone | all-reduce | flops 3072 | bytes 24576
  398.1 39.7 %psum.67 = f32[16,16]{1,0:T(8,128)S(1)} all-reduce(f32[16,16]{1,0:T(8,128)S(1)} %fusion.97), channel_id=1, replica_groups=mesh['cluster'=8,'sub'=4] {'cluster','sub'}, use_global_device_ids=true, to_apply=%region_12.0 | all-reduce | flops 256 | bytes 2048 | tf_op jit(solution)/shard_map/psum | solution.py:131
  455.6 4.5 collective-permute-done.14
  464.0 10.1 %all-reduce.8 = (f32[16,16]{1,0:T(8,128)S(1)}, f32[16,16]{0,1:T(8,128)S(1)}) all-reduce(f32[16,16]{1,0:T(8,128)S(1)} %fusion.90, f32[16,16]{0,1:T(8,128)S(1)} %fusion.92), channel_id=1, replica_groups=mesh['cluster'=8,'sub'=4] {'sub'}, use_global_device_ids=true, to_apply=%region_15.0 | all-reduce | flops 512 | bytes 4096 | tf_op jit(solution)/shard_map/psum | solution.py:91
  474.2 30.8 %all-reduce.6 = (f32[16,16]{1,0:T(8,128)S(1)}, f32[16,16]{0,1:T(8,128)S(1)}) all-reduce(f32[16,16]{1,0:T(8,128)S(1)} %get-tuple-element.12, f32[16,16]{0,1:T(8,128)S(1)} %get-tuple-element.13), channel_id=1, replica_groups=mesh['cluster'=8,'sub'=4] {'cluster'}, use_global_device_ids=true, to_apply=%region_16.0 | all-reduce | flops 512 | bytes 4096 | tf_op jit(solution)/shard_map/psum | solution.py:91
  514.1 41.6 %all-reduce.5 = f32[192,16]{0,1:T(8,128)S(1)} all-reduce(f32[192,16]{0,1:T(8,128)S(1)} %convolution_bitcast_fusion.11), channel_id=7, replica_groups=mesh['cluster'=8,'sub'=4] {'cluster','sub'}, use_global_device_ids=true, to_apply=%region_17.22.clone | all-reduce | flops 3072 | bytes 24576
  562.9 3.8 collective-permute-done.16
  (176 shorter events, 138.9 us)
Async XLA Ops:
  7.2 65.9 %copy-start = (f32[1,1,768,768]{3,2,1,0:T(8,128)S(1)}, f32[1,1,768,768]{3,2,1,0:T(8,128)}, u32[]{:S(2)}) copy-start(f32[1,1,768,768]{3,2,1,0:T(8,128)} %param.16) | copy-start | bytes 7077892
  7.2 44.1 %sort.19.cloned.1.call-start = ((), (), s32[]{:S(2)}) async-start(), calls=%async_computation | async-start | bytes 9248 | tf_op jit(solution)/shard_map/jit(argsort)/sort | solution.py:100
  56.5 28.5 %copy-start.2 = (f32[1,1,16,384]{3,2,1,0:T(8,128)S(1)}, f32[1,1,16,384]{3,2,1,0:T(8,128)}, u32[]{:S(2)}) copy-start(f32[1,1,16,384]{3,2,1,0:T(8,128)} %param.15) | copy-start | bytes 73732
  56.6 6.6 %collective-permute-start = (f32[1,1,16,384]{3,2,1,0:T(8,128)S(1)}, f32[1,1,16,384]{3,2,1,0:T(8,128)S(1)}, u32[]{:S(2)}, u32[]{:S(2)}) collective-permute-start(f32[1,1,16,384]{3,2,1,0:T(8,128)S(1)} %fusion.89), channel_id=1, source_target_pairs={{4,0},{8,4},{12,8},{16,12},{20,16},{24,20},{28,24},{5,1},{9,5},{13... | collective-permute-start | bytes 73736 | tf_op jit(solution)/shard_map/ppermute | solution.py:13
  63.3 5.7 collective-permute-start.1
  73.0 22.1 %copy-start.1 = (f32[6,192]{1,0:T(8,128)S(1)}, f32[6,192]{1,0:T(8,128)}, u32[]{:S(2)}) copy-start(f32[6,192]{1,0:T(8,128)} %param.22) | copy-start | bytes 13828
  73.1 70.6 %copy-start.3 = (f32[1,1,384]{2,1,0:T(1,128)S(1)}, f32[1,1,384]{2,1,0:T(1,128)}, u32[]{:S(2)}) copy-start(f32[1,1,384]{2,1,0:T(1,128)} %param.20) | copy-start | bytes 4612
  78.4 6.6 %collective-permute-start.2 = (f32[1,1,16,384]{3,2,1,0:T(8,128)S(1)}, f32[1,1,16,384]{3,2,1,0:T(8,128)S(1)}, u32[]{:S(2)}, u32[]{:S(2)}) collective-permute-start(f32[1,1,16,384]{3,2,1,0:T(8,128)S(1)} %fusion.87), channel_id=1, source_target_pairs={{4,0},{8,4},{12,8},{16,12},{20,16},{24,20},{28,24},{5,1},{9,5},{13... | collective-permute-start | bytes 73736 | tf_op jit(solution)/shard_map/ppermute | solution.py:13
  85.1 5.7 collective-permute-start.3
  141.2 6.6 %collective-permute-start.4 = (f32[1,1,16,384]{3,2,1,0:T(8,128)S(1)}, f32[1,1,16,384]{3,2,1,0:T(8,128)S(1)}, u32[]{:S(2)}, u32[]{:S(2)}) collective-permute-start(f32[1,1,16,384]{3,2,1,0:T(8,128)S(1)} %fusion.85), channel_id=1, source_target_pairs={{4,0},{8,4},{12,8},{16,12},{20,16},{24,20},{28,24},{5,1},{9,5},{13... | collective-permute-start | bytes 73736 | tf_op jit(solution)/shard_map/ppermute | solution.py:13
  147.8 5.7 collective-permute-start.5
  201.9 6.6 %collective-permute-start.6 = (f32[1,1,16,384]{3,2,1,0:T(8,128)S(1)}, f32[1,1,16,384]{3,2,1,0:T(8,128)S(1)}, u32[]{:S(2)}, u32[]{:S(2)}) collective-permute-start(f32[1,1,16,384]{3,2,1,0:T(8,128)S(1)} %fusion.83), channel_id=1, source_target_pairs={{4,0},{8,4},{12,8},{16,12},{20,16},{24,20},{28,24},{5,1},{9,5},{13... | collective-permute-start | bytes 73736 | tf_op jit(solution)/shard_map/ppermute | solution.py:13
  208.5 5.7 collective-permute-start.7
  223.6 6.6 %collective-permute-start.8 = (f32[1,1,16,384]{3,2,1,0:T(8,128)S(1)}, f32[1,1,16,384]{3,2,1,0:T(8,128)S(1)}, u32[]{:S(2)}, u32[]{:S(2)}) collective-permute-start(f32[1,1,16,384]{3,2,1,0:T(8,128)S(1)} %fusion.81), channel_id=1, source_target_pairs={{4,0},{8,4},{12,8},{16,12},{20,16},{24,20},{28,24},{5,1},{9,5},{13... | collective-permute-start | bytes 73736 | tf_op jit(solution)/shard_map/ppermute | solution.py:13
  230.4 48.6 %collective-permute-start.9 = (f32[1,1,16,384]{3,2,1,0:T(8,128)S(1)}, f32[1,1,16,384]{3,2,1,0:T(8,128)S(1)}, u32[]{:S(2)}, u32[]{:S(2)}) collective-permute-start(f32[1,1,16,384]{3,2,1,0:T(8,128)S(1)} %slice_add_fusion.4), channel_id=1, source_target_pairs={{0,4},{4,8},{8,12},{12,16},{16,20},{20,24},{24,28},{1,5},{5,9},{9,... | collective-permute-start | bytes 73736 | tf_op jit(solution)/shard_map/ppermute | solution.py:13
  328.8 6.6 %collective-permute-start.10 = (f32[1,1,16,384]{3,2,1,0:T(8,128)S(1)}, f32[1,1,16,384]{3,2,1,0:T(8,128)S(1)}, u32[]{:S(2)}, u32[]{:S(2)}) collective-permute-start(f32[1,1,16,384]{3,2,1,0:T(8,128)S(1)} %fusion.79), channel_id=1, source_target_pairs={{4,0},{8,4},{12,8},{16,12},{20,16},{24,20},{28,24},{5,1},{9,5},{13... | collective-permute-start | bytes 73736 | tf_op jit(solution)/shard_map/ppermute | solution.py:13
  335.6 5.7 collective-permute-start.11
  391.3 6.6 %collective-permute-start.12 = (f32[1,1,16,384]{3,2,1,0:T(8,128)S(1)}, f32[1,1,16,384]{3,2,1,0:T(8,128)S(1)}, u32[]{:S(2)}, u32[]{:S(2)}) collective-permute-start(f32[1,1,16,384]{3,2,1,0:T(8,128)S(1)} %fusion.77), channel_id=1, source_target_pairs={{4,0},{8,4},{12,8},{16,12},{20,16},{24,20},{28,24},{5,1},{9,5},{13... | collective-permute-start | bytes 73736 | tf_op jit(solution)/shard_map/ppermute | solution.py:13
  438.4 5.7 collective-permute-start.13
  453.5 6.6 %collective-permute-start.14 = (f32[1,1,16,384]{3,2,1,0:T(8,128)S(1)}, f32[1,1,16,384]{3,2,1,0:T(8,128)S(1)}, u32[]{:S(2)}, u32[]{:S(2)}) collective-permute-start(f32[1,1,16,384]{3,2,1,0:T(8,128)S(1)} %fusion.75), channel_id=1, source_target_pairs={{4,0},{8,4},{12,8},{16,12},{20,16},{24,20},{28,24},{5,1},{9,5},{13... | collective-permute-start | bytes 73736 | tf_op jit(solution)/shard_map/ppermute | solution.py:13
  460.3 49.3 %collective-permute-start.15 = (f32[1,1,16,384]{3,2,1,0:T(8,128)S(1)}, f32[1,1,16,384]{3,2,1,0:T(8,128)S(1)}, u32[]{:S(2)}, u32[]{:S(2)}) collective-permute-start(f32[1,1,16,384]{3,2,1,0:T(8,128)S(1)} %slice_add_fusion.1), channel_id=1, source_target_pairs={{0,4},{4,8},{8,12},{12,16},{16,20},{20,24},{24,28},{1,5},{5,9},{9,... | collective-permute-start | bytes 73736 | tf_op jit(solution)/shard_map/ppermute | solution.py:13
  560.1 6.6 %collective-permute-start.16 = (f32[1,1,16,384]{3,2,1,0:T(8,128)S(1)}, f32[1,1,16,384]{3,2,1,0:T(8,128)S(1)}, u32[]{:S(2)}, u32[]{:S(2)}) collective-permute-start(f32[1,1,16,384]{3,2,1,0:T(8,128)S(1)} %fusion.73), channel_id=1, source_target_pairs={{4,0},{8,4},{12,8},{16,12},{20,16},{24,20},{28,24},{5,1},{9,5},{13... | collective-permute-start | bytes 73736 | tf_op jit(solution)/shard_map/ppermute | solution.py:13
Sparse Core Ops, SparseCore 0:
  10.9 2.7 sort.21.cloned.1.call-done
  (1 shorter events, 0.0 us)
